TPU v7x, 256 devices: a whole 4x4x8 slice. The times are simulated.
256 devices in a mesh: mem: 8 (over x, core), gx: 4 (over z_hi), gy: 8 (over z_lo, y).
Axes of the slice: x: 4, y: 4, z: 8 (z_hi: 4, z_lo: 2; z = z_hi * 2 + z_lo), core: 2. Of those that a mesh axis runs over, the one named last changes fastest.
Arguments:
- prior_sample_set: float32 [256, 2, 256, 1024], P('mem', None, 'gx', 'gy'), may hold values from -6 to 6
- flow_speeds: float32 [2, 2, 256, 1024], P(None, None, 'gx', 'gy'), may hold values from -0.6 to 0.6
- observed_cells: int32 [4, 8, 8, 4, 128], P('gx', 'gy', 'mem'), may hold values from 0 to 511
- observed_values: float32 [4, 8, 8, 4, 128], P('gx', 'gy', 'mem'), may hold values from -6 to 6
- error_variance: float32 [4, 8, 8, 4, 128], P('gx', 'gy', 'mem'), may hold values from 0.5 to 4
Outputs:
- analysis: bfloat16 [256, 2, 256, 1024], P('mem', None, 'gx', 'gy')
All inputs are finite; a program needn't handle non-finite values.
Results may differ from a plain program's by a relative error of at most 0.001.
The roundings to bfloat16 on the way count: a program that leaves them out, or rounds other values in their place, can miss the bound.
Values may be sent and summed in bfloat16 or wider, within the bound.
A program may use at most 64 MiB of HBM per device.

v0:
```python
import functools

import jax
import jax.numpy as jnp
from jax import lax
from jax.experimental import pallas as pl
from jax.experimental.pallas import tpu as pltpu
from jax.sharding import PartitionSpec as P

MESH = pl.DeviceIdType.MESH
F32 = jnp.float32
BF16 = jnp.bfloat16

ROWS = 64
COLS = 128
LOCAL = 32
MEMS = 256
PEERS = 64
TOP = 8


def lanes_of(shape):
    return lax.broadcasted_iota(jnp.int32, shape, len(shape) - 1)


def roll(x, shift):
    shift = shift % COLS
    return x if shift == 0 else pltpu.roll(x, shift, x.ndim - 1)


def for_each_peer(mem, gy, body):
    def step(k, carry):
        other_mem, other_gy = lax.rem(k, 8), lax.div(k, 8)

        @pl.when(jnp.logical_or(other_mem != mem, other_gy != gy))
        def _():
            body(k, other_mem, other_gy)

        return carry

    lax.fori_loop(0, PEERS, step, 0)


def forecast_kernel(
    x_ref, w_ref, r_ref,
    u, v1, v2, v3, tu, t1, t2, t3,
    sends, dense, dense_in, corner_in,
    wide, packed, folded, folded_in, wind_corner_in, tw,
    coef, tcoef, out,
    h_send, h_recv, a_send, a_recv,
):
    mem, gx, gy = lax.axis_index("mem"), lax.axis_index("gx"), lax.axis_index("gy")
    up, down = lax.rem(gx + 1, 4), lax.rem(gx + 3, 4)
    east, west = lax.rem(gy + 1, 8), lax.rem(gy + 7, 8)
    me = gy * 8 + mem

    barrier = pltpu.get_barrier_semaphore()
    for other_gx in (up, down):
        for other_gy in (gy, east, west):
            pl.semaphore_signal(
                barrier, inc=1, device_id={"gx": other_gx, "gy": other_gy}, device_id_type=MESH
            )
    for_each_peer(
        mem, gy,
        lambda k, om, og: pl.semaphore_signal(
            barrier, inc=1, device_id={"mem": om, "gy": og}, device_id_type=MESH
        ),
    )

    lane = lanes_of((8, COLS))
    lane3 = lanes_of((8, 8, COLS))
    lane16 = lanes_of((16, 8, COLS))
    laneb = lanes_of((ROWS, COLS))
    lanec = lanes_of((16, COLS))

    edge = jnp.zeros((ROWS, COLS), F32)
    for q in range(4):
        wind = w_ref[q]
        wide[q, pl.ds(TOP, ROWS), :] = wind
        edge = jnp.where(laneb // 8 == q, roll(wind, 8 * q + 4), edge)
    packed[...] = edge
    fold = edge[0:16]
    for a in range(1, 4):
        fold = jnp.where(lanec // 32 == a, roll(edge[16 * a : 16 * a + 16], 32 * a), fold)
    folded[...] = fold

    def turn(rb, carry):
        edge = jnp.zeros((8, 8, COLS), F32)
        for l in range(2):
            for g in range(4):
                j = 4 * l + g
                block = x_ref[g * 8 : g * 8 + 8, l, pl.ds(rb * 8, 8), :]
                block = jnp.swapaxes(block, 0, 1)
                u[pl.ds(TOP + rb * 8, 8), l, g * 8 : g * 8 + 8, :] = block
                edge = jnp.where(lane3 // 8 == j, roll(block, 8 * j + 4), edge)
        sends[pl.ds(rb * 8, 8)] = edge
        return carry

    lax.fori_loop(0, 8, turn, 0)

    d0 = jnp.where(lane16 < 64, sends[0:16], roll(sends[32:48], 64))
    d1 = jnp.where(lane16 < 64, sends[16:32], roll(sends[48:64], 64))
    low16 = lax.rem(lane16, 8) < 4
    dense[0] = jnp.where(low16, d0, roll(d1, 4))
    dense[1] = jnp.where(low16, roll(d1, -4), d0)

    pl.semaphore_wait(barrier, PEERS - 1 + 6)

    plan = []

    def add(src, dst, device):
        i = len(plan)
        plan.append(
            pltpu.make_async_remote_copy(
                src_ref=src, dst_ref=dst, send_sem=h_send.at[i], recv_sem=h_recv.at[i],
                device_id=device, device_id_type=MESH,
            )
        )

    add(u.at[pl.ds(TOP + ROWS - 4, 4)], u.at[pl.ds(TOP - 4, 4)], {"gx": up})
    add(u.at[pl.ds(TOP, 4)], u.at[pl.ds(TOP + ROWS, 4)], {"gx": down})
    add(dense.at[0], dense_in.at[0], {"gy": east})
    add(dense.at[1], dense_in.at[1], {"gy": west})
    add(w_ref.at[:, pl.ds(ROWS - 8, 8), :], wide.at[:, pl.ds(0, 8), :], {"gx": up})
    add(w_ref.at[:, pl.ds(0, 8), :], wide.at[:, pl.ds(TOP + ROWS, 8), :], {"gx": down})
    add(folded, folded_in.at[0], {"gy": east})
    add(folded, folded_in.at[1], {"gy": west})
    corners = ((up, east, ROWS - 4, ROWS - 8), (up, west, ROWS - 4, ROWS - 8), (down, east, 0, 0), (down, west, 0, 0))
    for i, (cx, cy, row, wrow) in enumerate(corners):
        add(sends.at[pl.ds(row, 4)], corner_in.at[i], {"gx": cx, "gy": cy})
        add(packed.at[pl.ds(wrow, 8)], wind_corner_in.at[i], {"gx": cx, "gy": cy})
    for copy in plan:
        copy.start()
    for copy in plan:
        copy.wait()

    east_in, west_in = dense_in[0], dense_in[1]
    for a in range(4):
        right = 64 * (a // 2)
        left_part = roll(east_in, right - 4 * (a % 2))
        right_part = roll(west_in, right + 4 * (a % 2))
        tu[pl.ds(TOP + 16 * a, 16)] = jnp.where(low16, left_part, right_part)
    low4 = low16[0:4]
    tu[pl.ds(TOP - 4, 4)] = jnp.where(low4, corner_in[0], corner_in[1])
    tu[pl.ds(TOP + ROWS, 4)] = jnp.where(low4, corner_in[2], corner_in[3])

    lowc = lax.rem(lanec, 8) < 4
    low8 = lax.rem(lane, 8) < 4
    for a in range(4):
        tw[pl.ds(TOP + 16 * a, 16), :] = jnp.where(
            lowc, roll(folded_in[0], -32 * a), roll(folded_in[1], -32 * a)
        )
    tw[0:8, :] = jnp.where(low8, wind_corner_in[0], wind_corner_in[1])
    tw[pl.ds(TOP + ROWS, 8), :] = jnp.where(low8, wind_corner_in[2], wind_corner_in[3])

    lanew = lanes_of((80, COLS))
    tw_all = tw[...]
    for d in range(2):
        spread = jnp.zeros((80, COLS), F32)
        for j in range(8):
            spread = jnp.where(lanew // 8 == j, roll(tw_all, 8 * (j - (2 * d + j // 4))), spread)
        tcoef[2 * d] = 0.1 - 0.5 * spread
        tcoef[2 * d + 1] = 0.1 + 0.5 * spread
        for l in range(2):
            wind = wide[2 * d + l]
            coef[4 * l + 2 * d] = 0.1 - 0.5 * wind
            coef[4 * l + 2 * d + 1] = 0.1 + 0.5 * wind

    def row_of(ref, q, r):
        return jnp.broadcast_to(ref[q, pl.ds(r, 1), :], (8, COLS))

    def slopes(src, tsrc, r, with_edge):
        tc = tsrc[r]
        to_west, to_east = tc, tc
        centre = [[src[r, l, g * 8 : g * 8 + 8, :] for g in range(4)] for l in range(2)]
        result = [[None] * 4, [None] * 4]
        for l in range(2):
            an, as_, ae, aw = (row_of(coef, 4 * l + i, r) for i in range(4))
            for g in range(4):
                j = 4 * l + g
                c = centre[l][g]
                outside = roll(tc, 124 - 8 * j)
                w = roll(jnp.where(lane == COLS - 1, outside, c), 1)
                e = roll(jnp.where(lane == 0, outside, c), -1)
                if with_edge:
                    inside = roll(c, 8 * j + 4)
                    to_west = jnp.where(lane == 8 * j + 3, inside, to_west)
                    to_east = jnp.where(lane == 8 * j + 4, inside, to_east)
                n = src[r + 1, l, g * 8 : g * 8 + 8, :]
                s = src[r - 1, l, g * 8 : g * 8 + 8, :]
                result[l][g] = (
                    (an * n + as_ * s) + (ae * e + aw * w) + (0.1 * centre[1 - l][g] - 0.5 * c)
                )
        if not with_edge:
            return centre, result, None, None
        an, as_, ae, aw = (row_of(tcoef, i, r) for i in range(4))
        other = jnp.where(lane < 32, roll(tc, -32), roll(tc, 32))
        edge = (
            (an * tsrc[r + 1] + as_ * tsrc[r - 1])
            + (ae * roll(to_east, -1) + aw * roll(to_west, 1))
            + (0.1 * other - 0.5 * tc)
        )
        return centre, result, tc, edge

    def stage(src, tsrc, dst, tdst, alpha):
        def block(b, carry):
            for i in range(8):
                r = TOP - 4 + b * 8 + i
                _, result, _, edge = slopes(src, tsrc, r, True)
                for l in range(2):
                    for g in range(4):
                        dst[r, l, g * 8 : g * 8 + 8, :] = (
                            u[r, l, g * 8 : g * 8 + 8, :] + alpha * result[l][g]
                        )
                tdst[r] = tu[r] + alpha * edge
            return carry

        lax.fori_loop(0, 9, block, 0)

    stage(u, tu, v1, t1, 0.5)
    stage(v1, t1, v2, t2, 0.5)
    stage(v2, t2, v3, t3, 1.0)

    def piece(row, other_mem, other_gy, index):
        return pltpu.make_async_remote_copy(
            src_ref=out.at[row],
            dst_ref=r_ref.at[gy, :, pl.ds(pl.multiple_of(mem * LOCAL, LOCAL), LOCAL), :],
            send_sem=a_send.at[row], recv_sem=a_recv.at[index],
            device_id={"mem": other_mem, "gy": other_gy}, device_id_type=MESH,
        )

    def send_block(b):
        for i in range(8):
            row = b * 8 + i

            @pl.when(row != me)
            def _():
                piece(row, i, b, me).start()

    def last(k, carry):
        b = lax.rem(gy + k, 8)

        @pl.when(k > 0)
        def _():
            send_block(lax.rem(gy + k + 7, 8))

        for i in range(8):
            r = TOP + b * 8 + i
            centre, result, _, _ = slopes(v3, t3, r, False)
            for l in range(2):
                parts = []
                for g in range(4):
                    at = (r, l, slice(g * 8, g * 8 + 8), slice(None))
                    total = (v1[at] + 2.0 * v2[at]) + (centre[l][g] - u[at])
                    parts.append(total * (1.0 / 3.0) + result[l][g] * (1.0 / 6.0))
                out[b * 8 + i, l] = jnp.concatenate(parts, axis=0).astype(BF16)
        return carry

    lax.fori_loop(0, 8, last, 0)
    r_ref[gy, :, pl.ds(pl.multiple_of(mem * LOCAL, LOCAL), LOCAL), :] = out[me]
    send_block(lax.rem(gy + 7, 8))

    for_each_peer(mem, gy, lambda k, om, og: piece(k, om, og, k).wait_recv())
    for_each_peer(mem, gy, lambda k, om, og: piece(k, om, og, k).wait_send())


def forecast(x, winds):
    vm = pltpu.VMEM
    big = vm((80, 2, LOCAL, COLS), F32)
    thin = vm((80, 8, COLS), F32)
    return pl.pallas_call(
        forecast_kernel,
        out_shape=jax.ShapeDtypeStruct((8, 2, MEMS, COLS), BF16),
        in_specs=[pl.BlockSpec(memory_space=pltpu.VMEM)] * 2,
        out_specs=pl.BlockSpec(memory_space=pltpu.VMEM),
        scratch_shapes=[
            big, big, big, big, thin, thin, thin, thin,
            vm((ROWS, 8, COLS), F32), vm((2, 16, 8, COLS), F32), vm((2, 16, 8, COLS), F32),
            vm((4, 4, 8, COLS), F32),
            vm((4, 80, COLS), F32), vm((ROWS, COLS), F32), vm((16, COLS), F32),
            vm((2, 16, COLS), F32), vm((4, 8, COLS), F32), vm((80, COLS), F32),
            vm((8, 80, COLS), F32), vm((4, 80, COLS), F32), vm((ROWS, 2, LOCAL, COLS), BF16),
            pltpu.SemaphoreType.DMA((16,)), pltpu.SemaphoreType.DMA((16,)),
            pltpu.SemaphoreType.DMA((PEERS,)), pltpu.SemaphoreType.DMA((PEERS,)),
        ],
        compiler_params=pltpu.CompilerParams(collective_id=0, has_side_effects=True),
        name="forecast",
    )(x, winds)


def split(x):
    high = x.astype(BF16)
    return high, (x - high.astype(F32)).astype(BF16)


def dot(a, b, dims=((1,), (0,))):
    return lax.dot_general(a, b, (dims, ((), ())), preferred_element_type=F32)


def analysis_kernel(
    r_ref, cell_ref, value_ref, error_ref, o_ref,
    pert, mean, spread, innovation, weights, out, send_sem, recv_sem,
):
    mem, gy = lax.axis_index("mem"), lax.axis_index("gy")
    me = gy * 8 + mem
    barrier = pltpu.get_barrier_semaphore()
    for_each_peer(
        mem, gy,
        lambda k, om, og: pl.semaphore_signal(
            barrier, inc=1, device_id={"mem": om, "gy": og}, device_id_type=MESH
        ),
    )

    def centre(t, carry):
        for l in range(2):
            x = r_ref[t, l].astype(F32)
            mu = jnp.sum(x, axis=0, keepdims=True) * (1.0 / MEMS)
            mean[t, l : l + 1, :] = mu
            pert[t, :, l * COLS : (l + 1) * COLS] = (x - mu).astype(BF16)
        return carry

    lax.fori_loop(0, 8, centre, 0)

    site = lax.broadcasted_iota(jnp.int32, (COLS, COLS), 0)

    def observe(p, carry):
        cell = cell_ref[p]
        picked = jnp.zeros((MEMS, COLS), F32)
        for h in range(2):
            for l in range(2):
                chosen = jnp.where(site + (l * 256 + h * 128) == cell, 1.0, 0.0).astype(BF16)
                picked = picked + dot(r_ref[2 * p + h, l], chosen)
        base = jnp.sum(picked, axis=0, keepdims=True) * (1.0 / MEMS)
        spread[p] = picked - base
        innovation[p] = value_ref[p] - base
        return carry

    lax.fori_loop(0, 4, observe, 0)

    row = lax.broadcasted_iota(jnp.int32, (MEMS, MEMS), 0)
    column = lax.broadcasted_iota(jnp.int32, (MEMS, MEMS), 1)

    def times(a, b):
        return (dot(a[0], b[0]) + dot(a[0], b[1])) + dot(a[1], b[0])

    def unit(value):
        return jnp.where(row == column, value, 0.0)

    def solve(p, carry):
        parts = []
        projected = jnp.zeros((MEMS, 1), F32)
        for q in (-1, 0, 1):
            other = lax.rem(p + q + 4, 4)
            offset = lax.rem(cell_ref[other], 256).astype(F32) - 127.5
            distance = (q * 256 + offset) * (1.0 / 256.0)
            scale = jnp.sqrt(jnp.exp(-0.5 * distance * distance) / error_ref[other])
            part = spread[other] * scale
            projected = projected + jnp.sum(
                part * (innovation[other] * scale), axis=1, keepdims=True
            )
            parts.append(part)
        high, low = split(jnp.concatenate(parts, axis=1))
        both = ((1,), (1,))
        gram = (dot(high, high, both) + dot(high, low, both)) + dot(low, high, both) + unit(255.0)
        square = jnp.sum(
            jnp.sum(gram * gram, axis=0, keepdims=True), axis=1, keepdims=True
        )
        frob = jnp.sqrt(square)
        y = gram / frob
        middle = unit(1.5) - 0.5 * y
        z = split(middle)
        y = split(times(split(y), z))
        for step in range(1, 4):
            m = split(unit(1.5) - 0.5 * times(z, y))
            if step < 3:
                y = split(times(y, m))
                z = split(times(m, z))
            else:
                root = times(m, z)
        once = jnp.sum(root * projected, axis=0, keepdims=True)
        twice = jnp.sum(root * once, axis=1, keepdims=True)
        shift = jnp.sum(unit(twice), axis=0, keepdims=True) / frob
        weights[p] = (root * (jnp.sqrt(jnp.full((1, 1), 255.0, F32)) / jnp.sqrt(frob)) + shift).astype(BF16)
        return carry

    lax.fori_loop(0, 4, solve, 0)

    pl.semaphore_wait(barrier, PEERS - 1)

    def piece(t, other_mem, index):
        return pltpu.make_async_remote_copy(
            src_ref=out.at[t, :, pl.ds(pl.multiple_of(other_mem * LOCAL, LOCAL), LOCAL), :],
            dst_ref=o_ref.at[me],
            send_sem=send_sem.at[t * 8 + other_mem], recv_sem=recv_sem.at[index],
            device_id={"mem": other_mem, "gy": t}, device_id_type=MESH,
        )

    def send_tile(t):
        for i in range(8):

            @pl.when(t * 8 + i != me)
            def _():
                piece(t, i, me).start()

    position = lanes_of((1, MEMS)) % COLS

    def update(k, carry):
        t = lax.rem(gy + k, 8)

        @pl.when(k > 0)
        def _():
            send_tile(lax.rem(gy + k + 7, 8))

        s = lax.rem(lax.div(t + 7, 2), 4)
        half = 1 - lax.rem(t, 2)
        share = ((position + 128 * half).astype(F32) + 0.5) * (1.0 / 256.0)
        first = dot(weights[s], pert[t])
        second = dot(weights[lax.rem(s + 1, 4)], pert[t])
        increment = (1.0 - share) * first + share * second
        for l in range(2):
            out[t, l] = (
                increment[:, l * COLS : (l + 1) * COLS] + mean[t, l : l + 1, :]
            ).astype(BF16)
        return carry

    lax.fori_loop(0, 8, update, 0)
    o_ref[me] = out[gy, :, pl.ds(pl.multiple_of(mem * LOCAL, LOCAL), LOCAL), :]
    send_tile(lax.rem(gy + 7, 8))
    for_each_peer(mem, gy, lambda k, om, og: piece(og, om, k).wait_recv())
    for_each_peer(mem, gy, lambda k, om, og: piece(og, om, k).wait_send())


def analysis(strip, cells, values, errors):
    vm = pltpu.VMEM
    return pl.pallas_call(
        analysis_kernel,
        out_shape=jax.ShapeDtypeStruct((ROWS, 2, LOCAL, COLS), BF16),
        in_specs=[pl.BlockSpec(memory_space=pltpu.VMEM)] * 4,
        out_specs=pl.BlockSpec(memory_space=pltpu.VMEM),
        scratch_shapes=[
            vm((8, MEMS, MEMS), BF16), vm((8, 8, COLS), F32), vm((4, MEMS, COLS), F32),
            vm((4, 1, COLS), F32), vm((4, MEMS, MEMS), BF16), vm((8, 2, MEMS, COLS), BF16),
            pltpu.SemaphoreType.DMA((PEERS,)), pltpu.SemaphoreType.DMA((PEERS,)),
        ],
        compiler_params=pltpu.CompilerParams(collective_id=1, has_side_effects=True),
        name="analysis",
    )(strip, cells, values, errors)


def on_device(prior_sample_set, flow_speeds, observed_cells, observed_values, error_variance):
    strip = forecast(prior_sample_set, flow_speeds.reshape(4, ROWS, COLS))
    shape = (4, 1, COLS)
    result = analysis(
        strip,
        observed_cells.reshape(shape),
        observed_values.reshape(shape),
        error_variance.reshape(shape),
    )
    return jnp.transpose(result, (2, 1, 0, 3))


def solution(mesh):
    in_specs = (
        P("mem", None, "gx", "gy"),
        P(None, None, "gx", "gy"),
        P("gx", "gy", "mem", None, None),
        P("gx", "gy", "mem", None, None),
        P("gx", "gy", "mem", None, None),
    )
    out_specs = P("mem", None, "gx", "gy")
    return jax.shard_map(
        on_device, mesh=mesh, in_specs=in_specs, out_specs=out_specs, check_vma=False
    )
```

profile of v0, /device:TPU:31, one launch (start us, length us, event | category | flops | bytes accessed | tf_op | source)
XLA Modules:
  0.0 162.3 jit_solution(17157053804484377437)
XLA Ops:
  0.0 124.2 %forecast.1.r_ref = bf16[8,2,256,128]{3,2,1,0:T(8,128)(2,1)} custom-call(f32[32,2,64,128]{3,2,1,0:T(8,128)} %x_ref.1, f32[4,64,128]{2,1,0:T(8,128)} %bitcast.6), custom_call_target="tpu_custom_call" | custom-call | tf_op jit(solution)/shard_map/forecast/pallas_call | solution.py:271
  124.2 35.2 %analysis.1 = bf16[64,2,32,128]{3,2,1,0:T(8,128)(2,1)} custom-call(bf16[8,2,256,128]{3,2,1,0:T(8,128)(2,1)} %forecast.1.r_ref, s32[4,1,128]{2,1,0:T(1,128)} %bitcast.7, f32[4,1,128]{2,1,0:T(1,128)} %bitcast.8, f32[4,1,128]{2,1,0:T(1,128)} %bitcast.9), custom_call_target="tpu_custom_call" | custom-call | tf_op jit(solution)/shard_map/analysis/pallas_call | solution.py:435
  159.4 2.9 %copy.6 = bf16[32,2,64,128]{3,2,1,0:T(8,128)(2,1)} copy(bf16[32,2,64,128]{3,0,1,2:T(8,128)(2,1)} %bitcast.5) | data formatting | bytes 2097152 | tf_op jit(solution)/shard_map/transpose | solution.py:459
where the time goes:
time: 165 us; the launch traced here: 162 us
  Pallas kernels  159 us (96%)
  local copies, waits for them, and re-layouts  2.87 us (2%)
    pallas_call x1, Pallas kernels, forecast(): pl.pallas_call(forecast_kernel, out_shape=jax.ShapeDtypeStruct((8, 2, MEM...  124 us
    pallas_call x1, Pallas kernels, analysis(): pl.pallas_call(analysis_kernel, out_shape=jax.ShapeDtypeStruct((ROWS, 2,...  35.2 us

commit v1 on v0

--- a/solution.py
+++ b/solution.py
@@ -26,6 +26,16 @@
 def roll(x, shift):
     shift = shift % COLS
     return x if shift == 0 else pltpu.roll(x, shift, x.ndim - 1)
+
+
+def mirrored(low, low_shift, high, high_shift):
+    k_of = lanes_of(low.shape) % 8
+    result = None
+    for k in range(8):
+        source, shift = (high, high_shift) if k < 4 else (low, low_shift)
+        moved = roll(source, shift + 2 * k - 7)
+        result = moved if k == 0 else jnp.where(k_of == k, moved, result)
+    return result
 
 
 def for_each_peer(mem, gy, body):
@@ -134,24 +144,19 @@
     for copy in plan:
         copy.wait()
 
-    east_in, west_in = dense_in[0], dense_in[1]
     for a in range(4):
         right = 64 * (a // 2)
-        left_part = roll(east_in, right - 4 * (a % 2))
-        right_part = roll(west_in, right + 4 * (a % 2))
-        tu[pl.ds(TOP + 16 * a, 16)] = jnp.where(low16, left_part, right_part)
-    low4 = low16[0:4]
-    tu[pl.ds(TOP - 4, 4)] = jnp.where(low4, corner_in[0], corner_in[1])
-    tu[pl.ds(TOP + ROWS, 4)] = jnp.where(low4, corner_in[2], corner_in[3])
-
-    lowc = lax.rem(lanec, 8) < 4
-    low8 = lax.rem(lane, 8) < 4
+        for i in range(16):
+            tu[TOP + 16 * a + i] = mirrored(
+                dense_in[0, i], right - 4 * (a % 2), dense_in[1, i], right + 4 * (a % 2)
+            )
+    for i in range(4):
+        tu[TOP - 4 + i] = mirrored(corner_in[0, i], 0, corner_in[1, i], 0)
+        tu[TOP + ROWS + i] = mirrored(corner_in[2, i], 0, corner_in[3, i], 0)
     for a in range(4):
-        tw[pl.ds(TOP + 16 * a, 16), :] = jnp.where(
-            lowc, roll(folded_in[0], -32 * a), roll(folded_in[1], -32 * a)
-        )
-    tw[0:8, :] = jnp.where(low8, wind_corner_in[0], wind_corner_in[1])
-    tw[pl.ds(TOP + ROWS, 8), :] = jnp.where(low8, wind_corner_in[2], wind_corner_in[3])
+        tw[pl.ds(TOP + 16 * a, 16), :] = mirrored(folded_in[0], -32 * a, folded_in[1], -32 * a)
+    tw[0:8, :] = mirrored(wind_corner_in[0], 0, wind_corner_in[1], 0)
+    tw[pl.ds(TOP + ROWS, 8), :] = mirrored(wind_corner_in[2], 0, wind_corner_in[3], 0)
 
     lanew = lanes_of((80, COLS))
     tw_all = tw[...]
@@ -171,7 +176,8 @@
 
     def slopes(src, tsrc, r, with_edge):
         tc = tsrc[r]
-        to_west, to_east = tc, tc
+        if with_edge:
+            to_west, to_east = roll(tc, -1), roll(tc, 1)
         centre = [[src[r, l, g * 8 : g * 8 + 8, :] for g in range(4)] for l in range(2)]
         result = [[None] * 4, [None] * 4]
         for l in range(2):
@@ -179,9 +185,9 @@
             for g in range(4):
                 j = 4 * l + g
                 c = centre[l][g]
-                outside = roll(tc, 124 - 8 * j)
-                w = roll(jnp.where(lane == COLS - 1, outside, c), 1)
-                e = roll(jnp.where(lane == 0, outside, c), -1)
+                outside = roll(tc, -(8 * j + 4))
+                w = jnp.where(lane == 0, outside, roll(c, 1))
+                e = jnp.where(lane == COLS - 1, outside, roll(c, -1))
                 if with_edge:
                     inside = roll(c, 8 * j + 4)
                     to_west = jnp.where(lane == 8 * j + 3, inside, to_west)
@@ -197,7 +203,7 @@
         other = jnp.where(lane < 32, roll(tc, -32), roll(tc, 32))
         edge = (
             (an * tsrc[r + 1] + as_ * tsrc[r - 1])
-            + (ae * roll(to_east, -1) + aw * roll(to_west, 1))
+            + (ae * to_east + aw * to_west)
             + (0.1 * other - 0.5 * tc)
         )
         return centre, result, tc, edge

time: 165 us -> 95.3 us (0.58); the launches traced: 162 us -> 95.1 us
  Pallas kernels: 159 us -> 92.3 us
    pallas_call x1, Pallas kernels: 124 us -> 54.9 us  [forecast(): pl.pallas_call(forecast_kernel, out_shape=jax.ShapeDtypeStruct((8, 2, MEM...]
    pallas_call x1, Pallas kernels: 35.2 us -> 37.3 us  [analysis(): pl.pallas_call(analysis_kernel, out_shape=jax.ShapeDtypeStruct((ROWS, 2,...]
where the time goes in v1:
time: 95.3 us; the launch traced here: 95.1 us
  Pallas kernels  92.3 us (97%)
  local copies, waits for them, and re-layouts  2.87 us (3%)
    pallas_call x1, Pallas kernels, forecast(): pl.pallas_call(forecast_kernel, out_shape=jax.ShapeDtypeStruct((8, 2, MEM...  54.9 us
    pallas_call x1, Pallas kernels, analysis(): pl.pallas_call(analysis_kernel, out_shape=jax.ShapeDtypeStruct((ROWS, 2,...  37.3 us
    transpose x1, local copies, waits for them, and re-layouts, on_device(): return jnp.transpose(result, (2, 1, 0, 3))  2.87 us

profile of v1, /device:TPU:31, one launch (start us, length us, event | category | flops | bytes accessed | tf_op | source)
XLA Modules:
  0.0 95.1 jit_solution(17234837264253260457)
XLA Ops:
  0.0 54.9 %forecast.1.r_ref = bf16[8,2,256,128]{3,2,1,0:T(8,128)(2,1)} custom-call(f32[32,2,64,128]{3,2,1,0:T(8,128)} %x_ref.1, f32[4,64,128]{2,1,0:T(8,128)} %bitcast.6), custom_call_target="tpu_custom_call" | custom-call | tf_op jit(solution)/shard_map/forecast/pallas_call | solution.py:277
  55.0 37.3 %analysis.1 = bf16[64,2,32,128]{3,2,1,0:T(8,128)(2,1)} custom-call(bf16[8,2,256,128]{3,2,1,0:T(8,128)(2,1)} %forecast.1.r_ref, s32[4,1,128]{2,1,0:T(1,128)} %bitcast.7, f32[4,1,128]{2,1,0:T(1,128)} %bitcast.8, f32[4,1,128]{2,1,0:T(1,128)} %bitcast.9), custom_call_target="tpu_custom_call" | custom-call | tf_op jit(solution)/shard_map/analysis/pallas_call | solution.py:441
  92.3 2.9 %copy.6 = bf16[32,2,64,128]{3,2,1,0:T(8,128)(2,1)} copy(bf16[32,2,64,128]{3,0,1,2:T(8,128)(2,1)} %bitcast.5) | data formatting | bytes 2097152 | tf_op jit(solution)/shard_map/transpose | solution.py:465

commit v2 on v1

--- a/solution.py
+++ b/solution.py
@@ -51,12 +51,20 @@
     lax.fori_loop(0, PEERS, step, 0)
 
 
+def settle(pad):
+    def step(i, carry):
+        pad[...] = pad[...] * 0.5
+        return carry
+
+    lax.fori_loop(0, 40, step, 0)
+
+
 def forecast_kernel(
     x_ref, w_ref, r_ref,
     u, v1, v2, v3, tu, t1, t2, t3,
     sends, dense, dense_in, corner_in,
     wide, packed, folded, folded_in, wind_corner_in, tw,
-    coef, tcoef, out,
+    coef, tcoef, out, pad,
     h_send, h_recv, a_send, a_recv,
 ):
     mem, gx, gy = lax.axis_index("mem"), lax.axis_index("gx"), lax.axis_index("gy")
@@ -114,6 +122,7 @@
     dense[0] = jnp.where(low16, d0, roll(d1, 4))
     dense[1] = jnp.where(low16, roll(d1, -4), d0)
 
+    settle(pad)
     pl.semaphore_wait(barrier, PEERS - 1 + 6)
 
     plan = []
@@ -248,6 +257,7 @@
 
         @pl.when(k > 0)
         def _():
+            settle(pad)
             send_block(lax.rem(gy + k + 7, 8))
 
         for i in range(8):
@@ -264,6 +274,7 @@
 
     lax.fori_loop(0, 8, last, 0)
     r_ref[gy, :, pl.ds(pl.multiple_of(mem * LOCAL, LOCAL), LOCAL), :] = out[me]
+    settle(pad)
     send_block(lax.rem(gy + 7, 8))
 
     for_each_peer(mem, gy, lambda k, om, og: piece(k, om, og, k).wait_recv())
@@ -285,7 +296,7 @@
             vm((4, 4, 8, COLS), F32),
             vm((4, 80, COLS), F32), vm((ROWS, COLS), F32), vm((16, COLS), F32),
             vm((2, 16, COLS), F32), vm((4, 8, COLS), F32), vm((80, COLS), F32),
-            vm((8, 80, COLS), F32), vm((4, 80, COLS), F32), vm((ROWS, 2, LOCAL, COLS), BF16),
+            vm((8, 80, COLS), F32), vm((4, 80, COLS), F32), vm((ROWS, 2, LOCAL, COLS), BF16), vm((8, COLS), F32),
             pltpu.SemaphoreType.DMA((16,)), pltpu.SemaphoreType.DMA((16,)),
             pltpu.SemaphoreType.DMA((PEERS,)), pltpu.SemaphoreType.DMA((PEERS,)),
         ],
@@ -305,7 +316,7 @@
 
 def analysis_kernel(
     r_ref, cell_ref, value_ref, error_ref, o_ref,
-    pert, mean, spread, innovation, weights, out, send_sem, recv_sem,
+    pert, mean, spread, innovation, weights, out, pad, send_sem, recv_sem,
 ):
     mem, gy = lax.axis_index("mem"), lax.axis_index("gy")
     me = gy * 8 + mem
@@ -352,7 +363,7 @@
     def unit(value):
         return jnp.where(row == column, value, 0.0)
 
-    def solve(p, carry):
+    def solve(p):
         parts = []
         projected = jnp.zeros((MEMS, 1), F32)
         for q in (-1, 0, 1):
@@ -387,11 +398,6 @@
         twice = jnp.sum(root * once, axis=1, keepdims=True)
         shift = jnp.sum(unit(twice), axis=0, keepdims=True) / frob
         weights[p] = (root * (jnp.sqrt(jnp.full((1, 1), 255.0, F32)) / jnp.sqrt(frob)) + shift).astype(BF16)
-        return carry
-
-    lax.fori_loop(0, 4, solve, 0)
-
-    pl.semaphore_wait(barrier, PEERS - 1)
 
     def piece(t, other_mem, index):
         return pltpu.make_async_remote_copy(
@@ -410,28 +416,41 @@
 
     position = lanes_of((1, MEMS)) % COLS
 
-    def update(k, carry):
-        t = lax.rem(gy + k, 8)
+    def update(s):
+        tiles = []
+        for h in range(2):
+            half = lax.rem(gy + h, 2)
+            t = lax.rem(2 * s + 1 + half, 8)
+            share = ((position + 128 * half).astype(F32) + 0.5) * (1.0 / 256.0)
+            first = dot(weights[s], pert[t])
+            second = dot(weights[lax.rem(s + 1, 4)], pert[t])
+            increment = (1.0 - share) * first + share * second
+            for l in range(2):
+                out[t, l] = (
+                    increment[:, l * COLS : (l + 1) * COLS] + mean[t, l : l + 1, :]
+                ).astype(BF16)
+            tiles.append(t)
+        settle(pad)
+        for t in tiles:
+            send_tile(t)
+
+    def advance(k, carry):
+        @pl.when(k < 4)
+        def _():
+            solve(lax.rem(lax.div(gy, 2) + k, 4))
+
+        @pl.when(k == 0)
+        def _():
+            pl.semaphore_wait(barrier, PEERS - 1)
 
         @pl.when(k > 0)
         def _():
-            send_tile(lax.rem(gy + k + 7, 8))
-
-        s = lax.rem(lax.div(t + 7, 2), 4)
-        half = 1 - lax.rem(t, 2)
-        share = ((position + 128 * half).astype(F32) + 0.5) * (1.0 / 256.0)
-        first = dot(weights[s], pert[t])
-        second = dot(weights[lax.rem(s + 1, 4)], pert[t])
-        increment = (1.0 - share) * first + share * second
-        for l in range(2):
-            out[t, l] = (
-                increment[:, l * COLS : (l + 1) * COLS] + mean[t, l : l + 1, :]
-            ).astype(BF16)
-        return carry
-
-    lax.fori_loop(0, 8, update, 0)
+            update(lax.rem(lax.div(gy, 2) + k + 3, 4))
+
+        return carry
+
+    lax.fori_loop(0, 5, advance, 0)
     o_ref[me] = out[gy, :, pl.ds(pl.multiple_of(mem * LOCAL, LOCAL), LOCAL), :]
-    send_tile(lax.rem(gy + 7, 8))
     for_each_peer(mem, gy, lambda k, om, og: piece(og, om, k).wait_recv())
     for_each_peer(mem, gy, lambda k, om, og: piece(og, om, k).wait_send())
 
@@ -445,7 +464,7 @@
         out_specs=pl.BlockSpec(memory_space=pltpu.VMEM),
         scratch_shapes=[
             vm((8, MEMS, MEMS), BF16), vm((8, 8, COLS), F32), vm((4, MEMS, COLS), F32),
-            vm((4, 1, COLS), F32), vm((4, MEMS, MEMS), BF16), vm((8, 2, MEMS, COLS), BF16),
+            vm((4, 1, COLS), F32), vm((4, MEMS, MEMS), BF16), vm((8, 2, MEMS, COLS), BF16), vm((8, COLS), F32),
             pltpu.SemaphoreType.DMA((PEERS,)), pltpu.SemaphoreType.DMA((PEERS,)),
         ],
         compiler_params=pltpu.CompilerParams(collective_id=1, has_side_effects=True),

time: 95.3 us -> 94.1 us (0.987)
  Pallas kernels: 92.3 us -> 90.9 us
    pallas_call x1, Pallas kernels: 37.3 us -> 34.4 us  [analysis(): pl.pallas_call(analysis_kernel, out_shape=jax.ShapeDtypeStruct((ROWS, 2,...]
    pallas_call x1, Pallas kernels: 54.9 us -> 56.4 us  [forecast(): pl.pallas_call(forecast_kernel, out_shape=jax.ShapeDtypeStruct((8, 2, MEM...]
where the time goes in v2:
time: 94.1 us; the launch traced here: 93.7 us
  Pallas kernels  90.9 us (97%)
  local copies, waits for them, and re-layouts  2.87 us (3%)
    pallas_call x1, Pallas kernels, forecast(): pl.pallas_call(forecast_kernel, out_shape=jax.ShapeDtypeStruct((8, 2, MEM...  56.4 us
    pallas_call x1, Pallas kernels, analysis(): pl.pallas_call(analysis_kernel, out_shape=jax.ShapeDtypeStruct((ROWS, 2,...  34.4 us
    transpose x1, local copies, waits for them, and re-layouts, on_device(): return jnp.transpose(result, (2, 1, 0, 3))  2.87 us

profile of v2, /device:TPU:31, one launch (start us, length us, event | category | flops | bytes accessed | tf_op | source)
XLA Modules:
  0.0 93.7 jit_solution(12296422910825258509)
XLA Ops:
  0.0 56.4 %forecast.1.r_ref = bf16[8,2,256,128]{3,2,1,0:T(8,128)(2,1)} custom-call(f32[32,2,64,128]{3,2,1,0:T(8,128)} %x_ref.1, f32[4,64,128]{2,1,0:T(8,128)} %bitcast.6), custom_call_target="tpu_custom_call" | custom-call | tf_op jit(solution)/shard_map/forecast/pallas_call | solution.py:288
  56.4 34.4 %analysis.1 = bf16[64,2,32,128]{3,2,1,0:T(8,128)(2,1)} custom-call(bf16[8,2,256,128]{3,2,1,0:T(8,128)(2,1)} %forecast.1.r_ref, s32[4,1,128]{2,1,0:T(1,128)} %bitcast.7, f32[4,1,128]{2,1,0:T(1,128)} %bitcast.8, f32[4,1,128]{2,1,0:T(1,128)} %bitcast.9), custom_call_target="tpu_custom_call" | custom-call | tf_op jit(solution)/shard_map/analysis/pallas_call | solution.py:460
  90.9 2.9 %copy.6 = bf16[32,2,64,128]{3,2,1,0:T(8,128)(2,1)} copy(bf16[32,2,64,128]{3,0,1,2:T(8,128)(2,1)} %bitcast.5) | data formatting | bytes 2097152 | tf_op jit(solution)/shard_map/transpose | solution.py:484

commit v3 on v2

--- a/solution.py
+++ b/solution.py
@@ -217,24 +217,16 @@
         )
         return centre, result, tc, edge
 
-    def stage(src, tsrc, dst, tdst, alpha):
-        def block(b, carry):
-            for i in range(8):
-                r = TOP - 4 + b * 8 + i
-                _, result, _, edge = slopes(src, tsrc, r, True)
-                for l in range(2):
-                    for g in range(4):
-                        dst[r, l, g * 8 : g * 8 + 8, :] = (
-                            u[r, l, g * 8 : g * 8 + 8, :] + alpha * result[l][g]
-                        )
-                tdst[r] = tu[r] + alpha * edge
-            return carry
-
-        lax.fori_loop(0, 9, block, 0)
-
-    stage(u, tu, v1, t1, 0.5)
-    stage(v1, t1, v2, t2, 0.5)
-    stage(v2, t2, v3, t3, 1.0)
+    def stage(first, src, tsrc, dst, tdst, alpha):
+        for i in range(8):
+            r = first + i
+            _, result, _, edge = slopes(src, tsrc, r, True)
+            for l in range(2):
+                for g in range(4):
+                    dst[r, l, g * 8 : g * 8 + 8, :] = (
+                        u[r, l, g * 8 : g * 8 + 8, :] + alpha * result[l][g]
+                    )
+            tdst[r] = tu[r] + alpha * edge
 
     def piece(row, other_mem, other_gy, index):
         return pltpu.make_async_remote_copy(
@@ -252,14 +244,7 @@
             def _():
                 piece(row, i, b, me).start()
 
-    def last(k, carry):
-        b = lax.rem(gy + k, 8)
-
-        @pl.when(k > 0)
-        def _():
-            settle(pad)
-            send_block(lax.rem(gy + k + 7, 8))
-
+    def finish(b):
         for i in range(8):
             r = TOP + b * 8 + i
             centre, result, _, _ = slopes(v3, t3, r, False)
@@ -270,9 +255,40 @@
                     total = (v1[at] + 2.0 * v2[at]) + (centre[l][g] - u[at])
                     parts.append(total * (1.0 / 3.0) + result[l][g] * (1.0 / 6.0))
                 out[b * 8 + i, l] = jnp.concatenate(parts, axis=0).astype(BF16)
-        return carry
-
-    lax.fori_loop(0, 8, last, 0)
+
+    ahead = 8 - gy
+
+    def block_at(k):
+        second = k > ahead
+        block = jnp.where(second, k - ahead - 2, gy + k - 1)
+        return block, jnp.logical_or(k == 0, k == ahead + 1)
+
+    def advance(k, carry):
+        b, filling = block_at(k)
+        first = TOP + b * 8
+        stage(first + 3, u, tu, v1, t1, 0.5)
+        sent, no_send = block_at(k - 1)
+
+        @pl.when(jnp.logical_and(k > 0, jnp.logical_not(no_send)))
+        def _():
+            send_block(sent)
+
+        @pl.when(k + gy >= 0)
+        def _():
+            stage(first + 2, v1, t1, v2, t2, 0.5)
+
+        @pl.when(k + mem >= 0)
+        def _():
+            stage(first + 1, v2, t2, v3, t3, 1.0)
+
+        @pl.when(jnp.logical_not(filling))
+        def _():
+            finish(b)
+
+        return carry
+
+    steps = jnp.where(gy == 0, 9, 10)
+    lax.fori_loop(0, steps, advance, 0)
     r_ref[gy, :, pl.ds(pl.multiple_of(mem * LOCAL, LOCAL), LOCAL), :] = out[me]
     settle(pad)
     send_block(lax.rem(gy + 7, 8))

time: 94.1 us -> 89.8 us (0.954)
  Pallas kernels: 90.9 us -> 86.7 us
    pallas_call x1, Pallas kernels: 56.4 us -> 52.5 us  [forecast(): pl.pallas_call(forecast_kernel, out_shape=jax.ShapeDtypeStruct((8, 2, MEM...]
where the time goes in v3:
time: 89.8 us; the launch traced here: 89.6 us
  Pallas kernels  86.7 us (97%)
  local copies, waits for them, and re-layouts  2.87 us (3%)
    pallas_call x1, Pallas kernels, forecast(): pl.pallas_call(forecast_kernel, out_shape=jax.ShapeDtypeStruct((8, 2, MEM...  52.5 us
    pallas_call x1, Pallas kernels, analysis(): pl.pallas_call(analysis_kernel, out_shape=jax.ShapeDtypeStruct((ROWS, 2,...  34.3 us
    transpose x1, local copies, waits for them, and re-layouts, on_device(): return jnp.transpose(result, (2, 1, 0, 3))  2.87 us

profile of v3, /device:TPU:31, one launch (start us, length us, event | category | flops | bytes accessed | tf_op | source)
XLA Modules:
  0.0 89.6 jit_solution(17746563229202354166)
XLA Ops:
  0.0 52.5 %forecast.1.r_ref = bf16[8,2,256,128]{3,2,1,0:T(8,128)(2,1)} custom-call(f32[32,2,64,128]{3,2,1,0:T(8,128)} %x_ref.1, f32[4,64,128]{2,1,0:T(8,128)} %bitcast.6), custom_call_target="tpu_custom_call" | custom-call | tf_op jit(solution)/shard_map/forecast/pallas_call | solution.py:304
  52.5 34.3 %analysis.1 = bf16[64,2,32,128]{3,2,1,0:T(8,128)(2,1)} custom-call(bf16[8,2,256,128]{3,2,1,0:T(8,128)(2,1)} %forecast.1.r_ref, s32[4,1,128]{2,1,0:T(1,128)} %bitcast.7, f32[4,1,128]{2,1,0:T(1,128)} %bitcast.8, f32[4,1,128]{2,1,0:T(1,128)} %bitcast.9), custom_call_target="tpu_custom_call" | custom-call | tf_op jit(solution)/shard_map/analysis/pallas_call | solution.py:476
  86.8 2.9 %copy.6 = bf16[32,2,64,128]{3,2,1,0:T(8,128)(2,1)} copy(bf16[32,2,64,128]{3,0,1,2:T(8,128)(2,1)} %bitcast.5) | data formatting | bytes 2097152 | tf_op jit(solution)/shard_map/transpose | solution.py:500
